TPU v7x, 32 devices: a whole 2x2x4 slice. The times are simulated.
32 devices in a mesh: parts: 2 (over y), rng: 8 (over z, x), chan: 2 (over core).
Axes of the slice: x: 2, y: 2, z: 4, core: 2. Of those that a mesh axis runs over, the one named last changes fastest.
Arguments:
- snapshots: bfloat16 [8, 2, 16384, 192], P('parts', None, 'rng', 'chan'), parts along dimension 0, may hold values from -24 to 24
- train_gates: int32 [8, 128], P('parts', 'rng'), parts along dimension 0, may hold values from 0 to 2047
- guard_keep: int32 [8, 128], P('parts', 'rng'), parts along dimension 0, may hold values 0 or 1
- beam_cells: int32 [8, 16], P('parts'), parts along dimension 0, may hold values from 0 to 767
Outputs:
- beam_out: bfloat16 [8, 2, 16, 16384], P('parts', None, None, ('rng', 'chan')), parts along dimension 0
- weights: float32 [8, 16, 384], P('parts'), parts along dimension 0
There are 2 independent parts, one for each index of `parts`. A program takes and returns all parts, laid end to end along the dimension named above; each array names one. Nothing has to cross between parts.
Inputs may be any that keep to these rules, and one draw needn't show every extreme that they name: `train_gates`: an offset into the 2048 gates of the range group that holds the entry. `beam_cells`: angle cell times 12 plus Doppler cell.
All inputs are finite; a program needn't handle non-finite values. No bound on the sum of `guard_keep` on one device may be relied on, other than what follows from the above.
Results may differ from a plain program's by a relative error of at most 0.01225.
Values may be sent and summed in bfloat16 or wider, within the bound.
A program may use at most 64 MiB of HBM per device.

v0:
```python
import math

import jax
import jax.numpy as jnp
from jax import lax
from jax.sharding import PartitionSpec as P

ELEM = 16
PULSE = 12
CH = 192
ANGLES = 64


LOADING = 0.05


def steering(cells):
    angle_cell = (cells // PULSE).astype(jnp.float32)
    doppler_cell = (cells % PULSE).astype(jnp.float32)
    sine_angle = -1.0 + (2.0 * angle_cell + 1.0) / ANGLES
    doppler_freq = (doppler_cell + 0.5) / PULSE - 0.5
    channel = jnp.arange(CH, dtype=jnp.int32)
    element = (channel % ELEM).astype(jnp.float32)
    pulse_index = (channel // ELEM).astype(jnp.float32)
    phases = (
        math.pi * element[None, :] * sine_angle[:, None]
        + 2.0 * math.pi * pulse_index[None, :] * doppler_freq[:, None]
    )
    norm_scale = 1.0 / math.sqrt(CH)
    return jnp.concatenate([jnp.cos(phases), jnp.sin(phases)], axis=1) * norm_scale


def gram_product(left, right):
    return lax.dot_general(
        left, right, (((0,), (0,)), ((), ())), preferred_element_type=jnp.float32
    )


def apply_taps(beam_taps, samples):
    return lax.dot_general(
        beam_taps, samples, (((0,), (1,)), ((), ())), preferred_element_type=jnp.float32
    )


def solve_weights(covariance, steer_vec):
    matrix_order = covariance.shape[0]
    loading = LOADING * jnp.trace(covariance) / matrix_order + 1e-06
    loaded = covariance + loading * jnp.eye(matrix_order, dtype=jnp.float32)
    factor = jnp.linalg.cholesky(loaded)
    forward = lax.linalg.triangular_solve(factor, steer_vec.T, left_side=True, lower=True)
    solved = lax.linalg.triangular_solve(
        factor, forward, left_side=True, lower=True, transpose_a=True
    )
    unit_gain = jnp.sum(steer_vec.T * solved, axis=0)
    return (solved / unit_gain[None, :]).T


def make_taps(weight_rows):
    weights = weight_rows.T
    half_order = weights.shape[0] // 2
    rotated = jnp.concatenate([-weights[half_order:], weights[:half_order]], axis=0)
    return jnp.concatenate([weights, rotated], axis=1).astype(jnp.bfloat16)


def per_device(snapshots, train_gates, guard_keep, beam_cells):
    groups = snapshots.shape[0]
    shard_width = snapshots.shape[3]
    chan_count = lax.axis_size("chan")
    chan_place = lax.axis_index("chan")
    full_width = shard_width * chan_count
    beam_count = beam_cells.shape[1]
    picked = jax.vmap(lambda cube, chosen: jnp.take(cube, chosen, axis=1))(snapshots, train_gates)
    picked = picked * guard_keep[:, None, :, None].astype(jnp.bfloat16)
    training = lax.all_gather(picked, "chan", axis=3, tiled=True)
    training = lax.all_gather(training, "rng", axis=2, tiled=True)
    cov_list = []
    for bin_group in range(groups):
        chosen = training[bin_group]
        direct = jnp.concatenate([chosen[0], chosen[1]], axis=1)
        turned = jnp.concatenate([-chosen[1], chosen[0]], axis=1)
        covariance = gram_product(direct, direct) + gram_product(turned, turned)
        cov_list.append(covariance)
    cov_stack = jnp.stack(cov_list)
    steer_stack = jax.vmap(steering)(beam_cells)
    rng_place = lax.axis_index("rng")
    group_pick = rng_place % groups
    own_cov = lax.dynamic_index_in_dim(cov_stack, group_pick, 0, keepdims=False)
    own_steer = lax.dynamic_index_in_dim(steer_stack, group_pick, 0, keepdims=False)
    own_weights = solve_weights(own_cov, own_steer)
    group_ids = jnp.arange(groups, dtype=jnp.int32)
    owner = jnp.where((group_ids == group_pick) & (rng_place < groups), 1.0, 0.0).astype(
        jnp.float32
    )
    weight_stack = lax.psum(owner[:, None, None] * own_weights[None], "rng")
    taps_stack = jax.vmap(make_taps)(weight_stack)
    beam_list = []
    for bin_group in range(groups):
        beam_taps = taps_stack[bin_group]
        real_taps = lax.dynamic_slice_in_dim(beam_taps, chan_place * shard_width, shard_width, 0)
        imag_taps = lax.dynamic_slice_in_dim(
            beam_taps, full_width + chan_place * shard_width, shard_width, 0
        )
        partial_out = apply_taps(real_taps, snapshots[bin_group, 0]) + apply_taps(
            imag_taps, snapshots[bin_group, 1]
        )
        outputs = lax.psum_scatter(partial_out, "chan", scatter_dimension=1, tiled=True)
        beam_list.append(outputs.reshape(2, beam_count, outputs.shape[1]).astype(jnp.bfloat16))
    return (jnp.stack(beam_list), weight_stack)


def solution(mesh):
    placed = (
        P("parts", None, "rng", "chan"),
        P("parts", "rng"),
        P("parts", "rng"),
        P("parts", None),
    )
    return jax.shard_map(
        per_device,
        mesh=mesh,
        in_specs=placed,
        out_specs=(P("parts", None, None, ("rng", "chan")), P("parts", None, None)),
        check_vma=False,
    )
```

profile of v0, /device:TPU:0, one launch (start us, length us, event | category | flops | bytes accessed | tf_op | source)
XLA Modules:
  0.0 298.7 jit_solution(11843807177407830651)
XLA Ops:
  7.2 0.7 bitcast_or_fusion
  7.9 0.7 compare_and_fusion
  8.6 11.0 %copy.52 = bf16[4,2,2048,96]{3,1,2,0:T(2,128)(2,1)} copy(bf16[4,2,2048,96]{2,3,1,0:T(8,128)(2,1)} %param.4) | data formatting | bytes 6291456 | tf_op args[0]
  19.7 2.9 gather_fusion
  22.9 2.2 all_gather.6
  25.1 0.3 copy.55
  25.4 33.1 %all_gather.7 = bf16[4,2,128,192]{3,0,1,2:T(4,128)(2,1)S(1)} all-gather(bf16[4,2,16,192]{3,0,1,2:T(4,128)(2,1)S(1)} %copy.55), channel_id=1, replica_groups=mesh['parts'=2,'rng'=8,'chan'=2] {'rng'}, dimensions={2}, use_global_device_ids=true | all-gather | bytes 442368 | tf_op jit(solution)/shard_map/all_gather | solution.py:75
  58.5 0.8 fusion.132
  60.5 0.3 fusion.55
  60.7 0.3 fusion.3
  61.0 0.3 fusion.48
  61.3 0.3 fusion.2
  61.5 0.3 fusion.41
  61.8 0.3 fusion.1
  62.1 0.3 fusion.34
  62.3 0.3 fusion
  63.0 0.7 fusion.8
  64.7 11.7 %cholesky.76 = f32[128,128]{1,0:T(8,128)S(1)} custom-call(f32[128,128]{1,0:T(8,128)S(1)} %cholesky.189), custom_call_target="Cholesky" | custom-call | tf_op jit(solution)/shard_map/jit(cholesky)/cholesky | solution.py:49
  76.5 9.8 %custom-call.24 = f32[1,128,128]{1,2,0:T(8,128)S(1)} custom-call(f32[1,128,128]{2,1,0:T(8,128)S(1)} %get-tuple-element.51), custom_call_target="InvertDiagBlocksLowerTriangular" | custom-call | tf_op jit(solution)/shard_map/jit(cholesky)/cholesky | solution.py:49
  86.3 0.3 fusion.32
  86.6 0.3 convolution_subtract_fusion
  86.9 11.9 %cholesky.160 = f32[128,128]{1,0:T(8,128)S(1)} custom-call(f32[128,128]{1,0:T(8,128)S(1)} %cholesky.193), custom_call_target="Cholesky" | custom-call | tf_op jit(solution)/shard_map/jit(cholesky)/cholesky | solution.py:49
  99.1 9.8 %custom-call.25 = f32[1,128,128]{1,2,0:T(8,128)S(1)} custom-call(f32[1,128,128]{2,1,0:T(8,128)S(1)} %get-tuple-element.49), custom_call_target="InvertDiagBlocksLowerTriangular" | custom-call | tf_op jit(solution)/shard_map/jit(cholesky)/cholesky | solution.py:49
  109.0 0.3 convolution_dynamic-update-slice_fusion
  109.3 0.8 copy-done.1
  110.1 1.4 convolution_subtract_fusion.1
  111.5 11.7 %cholesky.179 = f32[128,128]{1,0:T(8,128)S(1)} custom-call(f32[128,128]{1,0:T(8,128)S(1)} %convolution_subtract_fusion.1), custom_call_target="Cholesky" | custom-call | tf_op jit(solution)/shard_map/jit(cholesky)/cholesky | solution.py:49
  123.4 0.6 compare_reduce_fusion
  124.0 0.6 constant_dynamic-update-slice_fusion.1
  124.6 0.7 compare_reduce_fusion.1
  127.2 1.9 select_select_fusion
  129.1 9.3 %while.1 = (s32[]{:T(128)}, f32[384,384]{0,1:T(8,128)}, s32[3,2]{0,1:T(2,128)S(1)}, f32[3,128,128]{2,1,0:T(8,128)S(1)}, s32[]{:T(128)}) while((s32[]{:T(128)}, f32[384,384]{0,1:T(8,128)}, s32[3,2]{0,1:T(2,128)S(1)}, f32[3,128,128]{2,1,0:T(8,128)S(1)}, s32[]{:T(128)}) %tuple.43), condition=%wide.while_cond, body=%wide.while_body.sunk | while | flops 2 | bytes 393321 | solution.py:51
  129.2 0.6 fusion.143
  129.8 2.3 dynamic-slice.15
  132.3 0.6 fusion.143
  132.9 2.3 dynamic-slice.15
  135.5 0.6 fusion.143
  136.1 2.3 dynamic-slice.15
  138.5 29.5 %custom-call.26 = f32[3,128,128]{1,2,0:T(8,128)S(1)} custom-call(f32[3,128,128]{2,1,0:T(8,128)S(1)} %get-tuple-element.9), custom_call_target="InvertDiagBlocksLowerTriangular" | custom-call | tf_op jit(solution)/shard_map/triangular_solve | solution.py:51
  168.0 0.3 fusion.69
  168.6 1.0 convolution_subtract_fusion.5
  169.8 1.1 convolution_subtract_fusion.4
  171.3 1.0 convolution_subtract_fusion.3
  172.5 1.1 convolution_subtract_fusion.2
  173.6 0.3 fusion.71
  174.1 0.7 broadcast_multiply_fusion
  174.9 71.2 %all-reduce.3.cloned.1.call-done = f32[4,16,384]{2,1,0:T(8,128)} async-done(((f32[4,16,384]{2,1,0:T(8,128)}), f32[4,16,384]{2,1,0:T(8,128)}) %all-reduce.3.cloned.1.call-update) | async-done | bytes 98320 | tf_op jit(solution)/shard_map/psum | solution.py:94
  246.1 0.9 bitcast_convert_fusion
  247.1 0.9 fusion.62
  248.3 1.0 convolution_add_fusion.3
  249.6 1.0 convolution_add_fusion.2
  250.7 0.3 fusion.13
  250.9 1.0 convolution_add_fusion.1
  252.2 1.0 convolution_add_fusion
  253.2 3.1 %reduce-scatter.5.cloned.1.call-done = f32[32,1024]{1,0:T(8,128)} async-done(((f32[32,2048]{1,0:T(8,128)}), f32[32,1024]{1,0:T(8,128)}) %reduce-scatter.5.cloned.1.call-update) | async-done | bytes 131088 | tf_op jit(solution)/shard_map/reduce_scatter | solution.py:106
  256.3 0.9 convert_element_type.85
  257.2 10.2 %reduce-scatter.7.cloned.1.call-done = f32[32,1024]{1,0:T(8,128)} async-done(((f32[32,2048]{1,0:T(8,128)}), f32[32,1024]{1,0:T(8,128)}) %reduce-scatter.7.cloned.1.call-update) | async-done | bytes 131088 | tf_op jit(solution)/shard_map/reduce_scatter | solution.py:106
  267.4 0.9 convert_element_type.87
  268.3 10.1 %reduce-scatter.9.cloned.1.call-done = f32[32,1024]{1,0:T(8,128)} async-done(((f32[32,2048]{1,0:T(8,128)}), f32[32,1024]{1,0:T(8,128)}) %reduce-scatter.9.cloned.1.call-update) | async-done | bytes 131088 | tf_op jit(solution)/shard_map/reduce_scatter | solution.py:106
  278.4 0.9 convert_element_type.89
  279.3 10.6 %reduce-scatter.11.cloned.1.call-done = f32[32,1024]{1,0:T(8,128)} async-done(((f32[32,2048]{1,0:T(8,128)}), f32[32,1024]{1,0:T(8,128)}) %reduce-scatter.11.cloned.1.call-update) | async-done | bytes 131088 | tf_op jit(solution)/shard_map/reduce_scatter | solution.py:106
  289.9 0.9 convert_element_type.91
  290.8 0.7 pad_maximum_fusion
  291.6 0.6 copy.96
  (84 shorter events, 5.7 us)
Async XLA Ops:
  7.2 239.0 %all-reduce.3.cloned.1.call-start = ((), (), s32[]{:S(2)}) async-start(), calls=%async_computation.4 | async-start | bytes 196608 | tf_op jit(solution)/shard_map/psum | solution.py:94
  8.6 14.0 %copy-start.5 = (s32[4,16]{1,0:T(4,128)S(1)}, s32[4,16]{1,0:T(4,128)}, u32[]{:S(2)}) copy-start(s32[4,16]{1,0:T(4,128)} %param.6) | copy-start | bytes 772
  64.7 44.3 %copy-start.2 = (f32[384,384]{1,0:T(8,128)}, f32[384,384]{1,0:T(8,128)S(1)}, u32[]{:S(2)}) copy-start(f32[384,384]{1,0:T(8,128)S(1)} %fusion.7) | copy-start | bytes 1769476
  86.6 81.4 %copy-start.4 = (s32[4,16]{1,0:T(4,128)S(1)}, s32[4,16]{1,0:T(4,128)}, u32[]{:S(2)}) copy-start(s32[4,16]{1,0:T(4,128)} %param.7) | copy-start | bytes 772
  109.3 0.8 copy-start.1
  110.1 138.0 %copy-start = (bf16[4,2,2048,96]{2,3,1,0:T(8,128)(2,1)S(1)}, bf16[4,2,2048,96]{2,3,1,0:T(8,128)(2,1)}, u32[]{:S(2)}) copy-start(bf16[4,2,2048,96]{2,3,1,0:T(8,128)(2,1)} %param.4) | copy-start | bytes 9437188
  174.9 81.4 %reduce-scatter.5.cloned.1.call-start = ((), (), s32[]{:S(2)}) async-start(), calls=%async_computation.5 | async-start | bytes 393216 | tf_op jit(solution)/shard_map/reduce_scatter | solution.py:106
  249.3 18.1 %reduce-scatter.7.cloned.1.call-start = ((), (), s32[]{:S(2)}) async-start(), calls=%async_computation.6 | async-start | bytes 393216 | tf_op jit(solution)/shard_map/reduce_scatter | solution.py:106
  249.6 41.9 %copy-start.3 = (f32[4,16,384]{2,1,0:T(8,128)S(1)}, f32[4,16,384]{2,1,0:T(8,128)}, u32[]{:S(2)}) copy-start(f32[4,16,384]{2,1,0:T(8,128)} %all-reduce.3.cloned.1.call-done) | copy-start | bytes 294916
  250.6 27.7 %reduce-scatter.9.cloned.1.call-start = ((), (), s32[]{:S(2)}) async-start(), calls=%async_computation.7 | async-start | bytes 393216 | tf_op jit(solution)/shard_map/reduce_scatter | solution.py:106
  251.9 38.0 %reduce-scatter.11.cloned.1.call-start = ((), (), s32[]{:S(2)}) async-start(), calls=%async_computation.8 | async-start | bytes 393216 | tf_op jit(solution)/shard_map/reduce_scatter | solution.py:106
Sparse Core Ops, SparseCore 0:
  175.0 71.1 all-reduce.2
  249.5 6.7 reduce-scatter.4
  258.5 8.8 reduce-scatter.6
  269.5 8.8 reduce-scatter.8
  281.0 8.8 reduce-scatter.10
where the time goes:
time: 300 us; the launch traced here: 299 us
  waiting for transfers between devices  105 us (35%)
  other arithmetic  97.9 us (33%)
  blocking collectives  35.3 us (12%)
  local copies, waits for them, and re-layouts  28.6 us (10%)
  between operations  16.8 us (6%)
  matrix products  14.6 us (5%)
    psum x1, waiting for transfers between devices, per_device(): weight_stack = lax.psum(owner[:, None, None] * own_weights[None], 'rng')  71.2 us
    another operation x10, other arithmetic, solve_weights(): factor = jnp.linalg.cholesky(loaded)  56.3 us
    reduce_scatter x4, waiting for transfers between devices, per_device(): lax.psum_scatter(partial_out, 'chan', scatter_dimension=1, tiled=True)  33.9 us
    all_gather x1, blocking collectives, per_device(): training = lax.all_gather(training, 'rng', axis=2, tiled=True)  33.1 us
    another operation x3, other arithmetic, solve_weights(): lax.linalg.triangular_solve(factor, forward, left_side=True, lower=True,...  31.4 us
    unnamed x22, local copies, waits for them, and re-layouts  13.5 us
    another operation x15, local copies, waits for them, and re-layouts  9.25 us
  transfers between devices with their start and end apart: 5, of which 5 were waited for; matrix products, arithmetic and copies ran while one was open for 2% of the time, Pallas kernels for 0%

commit v1 on v0

v1 whole, which is shorter than its diff:
```python
import functools
import math

import jax
import jax.numpy as jnp
from jax import lax
from jax.experimental import pallas as pl
from jax.experimental.pallas import tpu as pltpu
from jax.sharding import PartitionSpec as P

ELEM = 16
PULSE = 12
ANGLES = 64
LOADING = 0.05
LANES = 128
STEPS = 8
REFINE = 2

MESH = pl.DeviceIdType.MESH
F32 = jnp.float32
BF16 = jnp.bfloat16


def dot_nn(left, right):
    return lax.dot_general(left, right, (((1,), (0,)), ((), ())), preferred_element_type=F32)


def dot_nt(left, right):
    return lax.dot_general(left, right, (((1,), (1,)), ((), ())), preferred_element_type=F32)


def dot_tn(left, right):
    return lax.dot_general(left, right, (((0,), (0,)), ((), ())), preferred_element_type=F32)


def halves(value):
    high = value.astype(BF16)
    return high, (value - high.astype(F32)).astype(BF16)


def exact_dot(dot, value, right):
    rows = value.shape[0]
    high, rest = halves(value)
    middle = (value - high.astype(F32)).astype(BF16)
    low = (value - high.astype(F32) - middle.astype(F32)).astype(BF16)
    product = dot(jnp.concatenate([high, middle, low], axis=0), right)
    return product[:rows] + (product[rows : 2 * rows] + product[2 * rows :])


def turn(value, pad):
    pieces = []
    for base in range(0, value.shape[1], 2 * pad):
        pieces += [-value[:, base + pad : base + 2 * pad], value[:, base : base + pad]]
    return jnp.concatenate(pieces, axis=1)


def steer_rows(cells, beams, chans, width, pad):
    cell = jnp.zeros((beams, pad), F32)
    row = lax.broadcasted_iota(jnp.int32, (beams, pad), 0)
    for k in range(beams):
        cell = jnp.where(row == k, cells(k).astype(F32), cell)
    angle = jnp.floor((cell + 0.5) * (1.0 / PULSE))
    doppler = cell - PULSE * angle
    lane = lax.broadcasted_iota(jnp.int32, (beams, pad), 1)
    whole = 2.0 * ANGLES * PULSE / 4.0
    blocks = []
    for c in range(chans):
        channel = (lane + c * width).astype(F32)
        pulse = jnp.floor((channel + 0.5) * (1.0 / ELEM))
        element = channel - ELEM * pulse
        count = (PULSE / 4.0) * element * (2.0 * angle + 1.0 - ANGLES) + (ANGLES / 4.0) * pulse * (
            2.0 * doppler + 1.0 - PULSE
        )
        count = count - whole * jnp.floor(count * (1.0 / whole) + 0.5)
        phase = count * (2.0 * math.pi / whole)
        norm_scale = jnp.where(lane < width, 1.0 / math.sqrt(chans * width), 0.0)
        blocks += [jnp.cos(phase) * norm_scale, jnp.sin(phase) * norm_scale]
    return jnp.concatenate(blocks, axis=1)


def solve_rows(direct, steer, order, pad, store):
    train = direct.shape[0]
    dual = 2 * train <= direct.shape[1]
    both = jnp.concatenate([direct, turn(direct, pad)], axis=0)
    squares = direct.astype(F32)
    trace = 2.0 * jnp.sum(jnp.sum(squares * squares, axis=0, keepdims=True), axis=1, keepdims=True)
    loading = LOADING * trace / order + 1e-06
    span = 0.5 * trace * (1.0 + 1e-05) + 1e-06
    if dual:
        top = dot_nt(direct, both)

        def expand(rows):
            left, right = rows[:, :train], rows[:, train:]
            return jnp.concatenate([rows, jnp.concatenate([-right, left], axis=1)], axis=0)

    else:
        top = dot_tn(both, both)

        def expand(rows):
            return rows

    height, size = top.shape
    eye = jnp.where(
        lax.broadcasted_iota(jnp.int32, (height, size), 0)
        == lax.broadcasted_iota(jnp.int32, (height, size), 1),
        1.0,
        0.0,
    ).astype(F32)
    ratio = span / (span + 2.0 * loading)
    gap = top * (2.0 / span)

    def factors(ratio):
        scale = 2.0 / (2.0 - ratio * ratio)
        return scale * (1.0 + ratio), scale * ratio, ratio * ratio / (2.0 - ratio * ratio)

    def pair(high, low):
        high, low = expand(high), expand(low)
        return jnp.concatenate([high, low, high], axis=0)

    keep, drop, ratio = factors(ratio)
    start = 2.0 / (2.0 * loading + span)
    inverse = start * (keep * eye - drop * gap)
    high, low = halves(gap)
    square = dot_nn(jnp.concatenate([high, high, low], axis=1), pair(high, low))
    gap = 4.0 * gap - 2.0 * square

    def step(carry):
        gap, inverse, ratio = carry
        keep, drop, ratio = factors(ratio)
        high, low = halves(gap)
        inv_high, inv_low = halves(inverse)
        left = jnp.concatenate(
            [
                jnp.concatenate([high, high, low], axis=1),
                jnp.concatenate([inv_high, inv_high, inv_low], axis=1),
            ],
            axis=0,
        )
        product = dot_nn(left, pair(high, low))
        return (
            4.0 * gap - 2.0 * product[:height],
            keep * inverse - drop * product[height:],
            ratio,
        )

    carry = (gap, inverse, ratio)
    if dual:
        for _ in range(STEPS - 1):
            carry = step(carry)
    else:
        gap_store, inverse_store = store
        gap_store[...] = gap
        inverse_store[...] = inverse

        def body(_, ratio):
            new_gap, new_inverse, new_ratio = step((gap_store[...], inverse_store[...], ratio))
            gap_store[...] = new_gap
            inverse_store[...] = new_inverse
            return new_ratio

        ratio = lax.fori_loop(0, STEPS - 1, body, ratio)
        carry = (None, inverse_store[...], ratio)
    stacked = pair(*halves(carry[1]))

    def precondition(value):
        high, low = halves(value)
        return dot_nn(jnp.concatenate([high, high, low], axis=1), stacked)

    if dual:
        right = exact_dot(dot_nt, steer, both)
    else:
        right = steer
    answer = precondition(right)
    for _ in range(REFINE):
        if dual:
            image = exact_dot(dot_nt, exact_dot(dot_nn, answer, both), both)
        else:
            image = exact_dot(dot_nn, exact_dot(dot_nt, answer, both), both)
        answer = answer + precondition(right - loading * answer - image)
    if dual:
        answer = steer - exact_dot(dot_nn, answer, both)
    gain = jnp.sum(steer * answer, axis=1, keepdims=True)
    return answer / gain


def kernel(
    rng_count,
    chans,
    pad,
    snap,
    gates,
    guard,
    cells,
    out,
    weights_out,
    full,
    cube,
    piece,
    rows,
    taps_store,
    *rest,
):
    store, sems = rest[:-9], rest[-9:]
    full_sem, own_sem, half_send, half_recv, row_send, row_recv, row_own, tap_send, tap_recv = sems
    groups, _, width, span = snap.shape
    beams = weights_out.shape[1]
    train_dev = gates.shape[1]
    half = span // chans
    place = lax.axis_index("rng")
    chan = lax.axis_index("chan")
    mine = lax.rem(place, groups)
    cluster = place - mine

    loads = []
    for g in range(groups):
        load = pltpu.make_async_copy(snap.at[g], full.at[g], full_sem.at[g])
        load.start()
        loads.append(load)

    barrier = pltpu.get_barrier_semaphore()
    for d in range(rng_count):
        for e in range(chans):
            if d == 0 and e == 0:
                continue
            pl.semaphore_signal(
                barrier,
                inc=1,
                device_id={
                    "rng": lax.rem(place + d, rng_count),
                    "chan": lax.rem(chan + e, chans),
                },
                device_id_type=MESH,
            )

    own_start = pl.multiple_of(chan * half, LANES)
    owns = []
    for g in range(groups):
        own = pltpu.make_async_copy(
            snap.at[g, :, :, pl.ds(own_start, half)],
            cube.at[g, chan, :, pl.ds(0, width), :],
            own_sem.at[g],
        )
        own.start()
        owns.append(own)
    if pad > width:
        for g in range(groups):
            for c in range(chans):
                for q in range(2):
                    cube[g, c, q, pl.ds(width, pad - width), :] = jnp.zeros(
                        (pad - width, half), BF16
                    )
    piece[...] = jnp.zeros_like(piece)
    steer = steer_rows(lambda k: cells[mine, k], beams, chans, width, pad)

    row = lax.broadcasted_iota(jnp.int32, (train_dev, LANES), 0)
    lane = lax.broadcasted_iota(jnp.int32, (train_dev, LANES), 1)
    for g in range(groups):
        chosen = jnp.full((train_dev, LANES), -1, jnp.int32)
        for t in range(train_dev):
            chosen = jnp.where(
                row == t, jnp.where(guard[g, t] != 0, gates[g, t], -1), chosen
            )
        offset = chosen - lane
        onehot = jnp.concatenate(
            [
                jnp.where(offset == base, 1.0, 0.0).astype(BF16)
                for base in range(0, span, LANES)
            ],
            axis=1,
        )
        loads[g].wait()
        for q in range(2):
            piece[g, :, pl.ds(q * pad, width)] = dot_nt(onehot, full[g, q]).astype(BF16)

    pl.semaphore_wait(barrier, rng_count * chans - 1)

    row_copies = []
    for d in range(rng_count - 1, -1, -1):
        target = lax.rem(place + d, rng_count)
        for e in range(chans):
            if d == 0 and e == 0:
                continue
            copy = pltpu.make_async_remote_copy(
                src_ref=piece.at[lax.rem(target, groups)],
                dst_ref=rows.at[place, chan],
                send_sem=row_send.at[d, e],
                recv_sem=row_recv.at[place, chan],
                device_id={"rng": target, "chan": lax.rem(chan + e, chans)},
                device_id_type=MESH,
            )
            copy.start()
            row_copies.append(copy)
    own_rows = pltpu.make_async_copy(piece.at[mine], rows.at[place, chan], row_own)
    own_rows.start()

    half_copies = []
    for g in range(groups):
        for e in range(1, chans):
            other = lax.rem(chan + e, chans)
            copy = pltpu.make_async_remote_copy(
                src_ref=snap.at[g, :, :, pl.ds(pl.multiple_of(other * half, LANES), half)],
                dst_ref=cube.at[g, chan, :, pl.ds(0, width), :],
                send_sem=half_send.at[g, e],
                recv_sem=half_recv.at[g, e],
                device_id={"chan": other},
                device_id_type=MESH,
            )
            copy.start()
            half_copies.append(copy)

    own_rows.wait()
    for d in range(rng_count):
        source = lax.rem(place + d, rng_count)
        for e in range(chans):
            if d == 0 and e == 0:
                continue
            from_chan = lax.rem(chan + e, chans)
            pltpu.make_async_copy(
                rows.at[source, from_chan],
                rows.at[source, from_chan],
                row_recv.at[source, from_chan],
            ).wait()

    direct = jnp.concatenate(
        [rows[:, c].reshape(rng_count * train_dev, 2 * pad) for c in range(chans)], axis=1
    )
    taps_store[mine] = solve_rows(direct, steer, 2 * chans * width, pad, store)

    tap_copies = []
    for d in range(1, groups):
        copy = pltpu.make_async_remote_copy(
            src_ref=taps_store.at[mine],
            dst_ref=taps_store.at[mine],
            send_sem=tap_send.at[d],
            recv_sem=tap_recv.at[mine],
            device_id={"rng": cluster + lax.rem(mine + d, groups)},
            device_id_type=MESH,
        )
        copy.start()
        tap_copies.append(copy)

    for own in owns:
        own.wait()
    for copy in half_copies:
        copy.wait()
    for d in range(groups):
        g = lax.rem(mine + d, groups)
        if d > 0:
            pltpu.make_async_copy(taps_store.at[g], taps_store.at[g], tap_recv.at[g]).wait()
        weights = taps_store[g]
        taps = jnp.concatenate([weights, turn(weights, pad)], axis=0).astype(BF16)
        samples = cube[g].reshape(chans * 2 * pad, half)
        out[g] = dot_nn(taps, samples).astype(BF16).reshape(2, beams, half)
        weights_out[g] = jnp.concatenate(
            [
                weights[:, c * 2 * pad + q * pad : c * 2 * pad + q * pad + width]
                for q in range(2)
                for c in range(chans)
            ],
            axis=1,
        )
    for copy in row_copies:
        copy.wait_send()
    for copy in tap_copies:
        copy.wait_send()


def per_device(rng_count, chans, snapshots, train_gates, guard_keep, beam_cells):
    groups, _, span, width = snapshots.shape
    beams = beam_cells.shape[1]
    train_dev = train_gates.shape[1]
    pad = -(-width // LANES) * LANES
    half = span // chans
    lanes = chans * 2 * pad
    store = []
    if 2 * rng_count * train_dev > lanes:
        store = [pltpu.VMEM((lanes, lanes), F32), pltpu.VMEM((lanes, lanes), F32)]
    dma = pltpu.SemaphoreType.DMA
    return pl.pallas_call(
        functools.partial(kernel, rng_count, chans, pad),
        out_shape=(
            jax.ShapeDtypeStruct((groups, 2, beams, half), BF16),
            jax.ShapeDtypeStruct((groups, beams, chans * 2 * width), F32),
        ),
        in_specs=[
            pl.BlockSpec(memory_space=pl.ANY),
            pl.BlockSpec(memory_space=pltpu.SMEM),
            pl.BlockSpec(memory_space=pltpu.SMEM),
            pl.BlockSpec(memory_space=pltpu.SMEM),
        ],
        out_specs=(
            pl.BlockSpec(memory_space=pltpu.VMEM),
            pl.BlockSpec(memory_space=pltpu.VMEM),
        ),
        scratch_shapes=[
            pltpu.VMEM((groups, 2, width, span), BF16),
            pltpu.VMEM((groups, chans, 2, pad, half), BF16),
            pltpu.VMEM((groups, train_dev, 2 * pad), BF16),
            pltpu.VMEM((rng_count, chans, train_dev, 2 * pad), BF16),
            pltpu.VMEM((groups, beams, lanes), F32),
            *store,
            dma((groups,)),
            dma((groups,)),
            dma((groups, chans)),
            dma((groups, chans)),
            dma((rng_count, chans)),
            dma((rng_count, chans)),
            dma,
            dma((groups,)),
            dma((groups,)),
        ],
        compiler_params=pltpu.CompilerParams(
            collective_id=0, has_side_effects=True, vmem_limit_bytes=56 * 1024 * 1024
        ),
    )(jnp.transpose(snapshots, (0, 1, 3, 2)), train_gates, guard_keep, beam_cells)


def solution(mesh):
    placed = (
        P("parts", None, "rng", "chan"),
        P("parts", "rng"),
        P("parts", "rng"),
        P("parts", None),
    )
    return jax.shard_map(
        functools.partial(per_device, mesh.shape["rng"], mesh.shape["chan"]),
        mesh=mesh,
        in_specs=placed,
        out_specs=(P("parts", None, None, ("rng", "chan")), P("parts", None, None)),
        check_vma=False,
    )
```

time: 300 us -> 25.1 us (0.08)
  waiting for transfers between devices: 105 us -> 0 us
  other arithmetic: 97.9 us -> 0 us
  blocking collectives: 35.3 us -> 0 us
  local copies, waits for them, and re-layouts: 28.6 us -> 3.21 us
  Pallas kernels: 0 us -> 21.1 us
  between operations: 16.8 us -> 0.64 us
  matrix products: 14.6 us -> 0 us
    another operation x17 -> x0, other arithmetic: 90.5 us -> none  [the longest x10 56.3 us: solve_weights(): factor = jnp.linalg.cholesky(loaded)]
    psum x1 -> x0, waiting for transfers between devices: 71.2 us -> none  [per_device(): weight_stack = lax.psum(owner[:, None, None] * own_weights[None], 'rng')]
    all_gather x2 -> x0, blocking collectives: 35.3 us -> none  [the longest x1 33.1 us: per_device(): training = lax.all_gather(training, 'rng', axis=2, tiled=True)]
    reduce_scatter x4 -> x0, waiting for transfers between devices: 33.9 us -> none  [per_device(): lax.psum_scatter(partial_out, 'chan', scatter_dimension=1, tiled=True)]
    pallas_call x0 -> x1, Pallas kernels: none -> 21.1 us  [per_device(): pl.pallas_call(functools.partial(kernel, rng_count, chans, pad), out_shap...]
    another operation x26 -> x0, local copies, waits for them, and re-layouts: 10.3 us -> none
    unnamed x22 -> x2, local copies, waits for them, and re-layouts: 13.5 us -> 3.21 us
    another operation x14 -> x0, matrix products: 7.66 us -> none  [the longest x5 2.86 us: solve_weights(): lax.linalg.triangular_solve(factor, forward, left_side=True, lower=True,...]
  transfers between devices with their start and end apart: 5 -> 0, of which waited for: 5 -> 0; matrix products, arithmetic and copies ran while one was open for 2% -> 0% of each run, Pallas kernels for 0% -> 0%
where the time goes in v1:
time: 25.1 us; the launch traced here: 24.9 us
  Pallas kernels  21.1 us (84%)
  local copies, waits for them, and re-layouts  3.21 us (13%)
  between operations  0.64 us (3%)
    pallas_call x1, Pallas kernels, per_device(): pl.pallas_call(functools.partial(kernel, rng_count, chans, pad), out_shap...  21.1 us
    unnamed x2, local copies, waits for them, and re-layouts  3.21 us

profile of v1, /device:TPU:0, one launch (start us, length us, event | category | flops | bytes accessed | tf_op | source)
XLA Modules:
  0.0 24.9 jit_solution(9829541265639119540)
XLA Ops:
  0.6 21.1 %shard_map.59 = (bf16[4,2,16,1024]{3,2,1,0:T(8,128)(2,1)}, f32[4,16,384]{2,1,0:T(8,128)}) custom-call(bf16[4,2,96,2048]{3,2,1,0:T(8,128)(2,1)} %bitcast.1, s32[4,16]{1,0:T(4,128)} %gates.1, s32[4,16]{1,0:T(4,128)} %guard.1, s32[4,16]{1,0:T(4,128)} %cells.1), custom_call_target="tpu_custom_call" | custom-call | tf_op jit(solution)/shard_map/pallas_call | solution.py:379
  21.7 1.7 %copy.8 = bf16[4,2,16,1024]{3,2,1,0:T(8,128)(2,1)} copy(bf16[4,2,16,1024]{3,2,1,0:T(8,128)(2,1)} %get-tuple-element.4) | data formatting | bytes 524288
  23.4 1.5 %copy.9 = f32[4,16,384]{2,1,0:T(8,128)} copy(f32[4,16,384]{2,1,0:T(8,128)} %get-tuple-element.5) | data formatting | bytes 196608

commit v2 on v1

--- a/solution.py
+++ b/solution.py
@@ -14,7 +14,7 @@
 LOADING = 0.05
 LANES = 128
 STEPS = 8
-REFINE = 2
+REFINE = 3
 
 MESH = pl.DeviceIdType.MESH
 F32 = jnp.float32
@@ -197,7 +197,6 @@
     cube,
     piece,
     rows,
-    taps_store,
     *rest,
 ):
     store, sems = rest[:-9], rest[-9:]
@@ -208,8 +207,10 @@
     half = span // chans
     place = lax.axis_index("rng")
     chan = lax.axis_index("chan")
-    mine = lax.rem(place, groups)
-    cluster = place - mine
+    chips = groups // chans
+    spot = lax.rem(place, chips)
+    mine = spot * chans + chan
+    cluster = place - spot
 
     loads = []
     for g in range(groups):
@@ -237,18 +238,11 @@
     for g in range(groups):
         own = pltpu.make_async_copy(
             snap.at[g, :, :, pl.ds(own_start, half)],
-            cube.at[g, chan, :, pl.ds(0, width), :],
+            cube.at[g, :, chan],
             own_sem.at[g],
         )
         own.start()
         owns.append(own)
-    if pad > width:
-        for g in range(groups):
-            for c in range(chans):
-                for q in range(2):
-                    cube[g, c, q, pl.ds(width, pad - width), :] = jnp.zeros(
-                        (pad - width, half), BF16
-                    )
     piece[...] = jnp.zeros_like(piece)
     steer = steer_rows(lambda k: cells[mine, k], beams, chans, width, pad)
 
@@ -280,12 +274,13 @@
         for e in range(chans):
             if d == 0 and e == 0:
                 continue
+            to_chan = lax.rem(chan + e, chans)
             copy = pltpu.make_async_remote_copy(
-                src_ref=piece.at[lax.rem(target, groups)],
+                src_ref=piece.at[lax.rem(target, chips) * chans + to_chan],
                 dst_ref=rows.at[place, chan],
                 send_sem=row_send.at[d, e],
                 recv_sem=row_recv.at[place, chan],
-                device_id={"rng": target, "chan": lax.rem(chan + e, chans)},
+                device_id={"rng": target, "chan": to_chan},
                 device_id_type=MESH,
             )
             copy.start()
@@ -299,7 +294,7 @@
             other = lax.rem(chan + e, chans)
             copy = pltpu.make_async_remote_copy(
                 src_ref=snap.at[g, :, :, pl.ds(pl.multiple_of(other * half, LANES), half)],
-                dst_ref=cube.at[g, chan, :, pl.ds(0, width), :],
+                dst_ref=cube.at[g, :, chan],
                 send_sem=half_send.at[g, e],
                 recv_sem=half_recv.at[g, e],
                 device_id={"chan": other},
@@ -324,41 +319,53 @@
     direct = jnp.concatenate(
         [rows[:, c].reshape(rng_count * train_dev, 2 * pad) for c in range(chans)], axis=1
     )
-    taps_store[mine] = solve_rows(direct, steer, 2 * chans * width, pad, store)
+    weights = solve_rows(direct, steer, 2 * chans * width, pad, store)
+    weights_out[mine] = jnp.concatenate(
+        [
+            weights[:, c * 2 * pad + q * pad : c * 2 * pad + q * pad + width]
+            for q in range(2)
+            for c in range(chans)
+        ],
+        axis=1,
+    )
 
     tap_copies = []
-    for d in range(1, groups):
-        copy = pltpu.make_async_remote_copy(
-            src_ref=taps_store.at[mine],
-            dst_ref=taps_store.at[mine],
-            send_sem=tap_send.at[d],
-            recv_sem=tap_recv.at[mine],
-            device_id={"rng": cluster + lax.rem(mine + d, groups)},
-            device_id_type=MESH,
-        )
-        copy.start()
-        tap_copies.append(copy)
+    for d in range(chips - 1, -1, -1):
+        for e in range(chans):
+            if d == 0 and e == 0:
+                continue
+            copy = pltpu.make_async_remote_copy(
+                src_ref=weights_out.at[mine],
+                dst_ref=weights_out.at[mine],
+                send_sem=tap_send.at[d, e],
+                recv_sem=tap_recv.at[mine],
+                device_id={
+                    "rng": cluster + lax.rem(spot + d, chips),
+                    "chan": lax.rem(chan + e, chans),
+                },
+                device_id_type=MESH,
+            )
+            copy.start()
+            tap_copies.append(copy)
 
     for own in owns:
         own.wait()
     for copy in half_copies:
         copy.wait()
-    for d in range(groups):
-        g = lax.rem(mine + d, groups)
-        if d > 0:
-            pltpu.make_async_copy(taps_store.at[g], taps_store.at[g], tap_recv.at[g]).wait()
-        weights = taps_store[g]
-        taps = jnp.concatenate([weights, turn(weights, pad)], axis=0).astype(BF16)
-        samples = cube[g].reshape(chans * 2 * pad, half)
-        out[g] = dot_nn(taps, samples).astype(BF16).reshape(2, beams, half)
-        weights_out[g] = jnp.concatenate(
-            [
-                weights[:, c * 2 * pad + q * pad : c * 2 * pad + q * pad + width]
-                for q in range(2)
-                for c in range(chans)
-            ],
-            axis=1,
-        )
+    for d in range(chips):
+        for e in range(chans):
+            g = lax.rem(spot + d, chips) * chans + lax.rem(chan + e, chans)
+            if d > 0 or e > 0:
+                pltpu.make_async_copy(
+                    weights_out.at[g], weights_out.at[g], tap_recv.at[g]
+                ).wait()
+            weights = weights_out[g]
+            turned = jnp.concatenate(
+                [-weights[:, chans * width :], weights[:, : chans * width]], axis=1
+            )
+            taps = jnp.concatenate([weights, turned], axis=0).astype(BF16)
+            samples = cube[g].reshape(2 * chans * width, half)
+            out[g] = dot_nn(taps, samples).astype(BF16).reshape(2, beams, half)
     for copy in row_copies:
         copy.wait_send()
     for copy in tap_copies:
@@ -376,11 +383,11 @@
     if 2 * rng_count * train_dev > lanes:
         store = [pltpu.VMEM((lanes, lanes), F32), pltpu.VMEM((lanes, lanes), F32)]
     dma = pltpu.SemaphoreType.DMA
-    return pl.pallas_call(
+    results = pl.pallas_call(
         functools.partial(kernel, rng_count, chans, pad),
         out_shape=(
-            jax.ShapeDtypeStruct((groups, 2, beams, half), BF16),
-            jax.ShapeDtypeStruct((groups, beams, chans * 2 * width), F32),
+            pltpu.VMEM((groups, 2, beams, half), BF16),
+            pltpu.VMEM((groups, beams, chans * 2 * width), F32),
         ),
         in_specs=[
             pl.BlockSpec(memory_space=pl.ANY),
@@ -394,10 +401,9 @@
         ),
         scratch_shapes=[
             pltpu.VMEM((groups, 2, width, span), BF16),
-            pltpu.VMEM((groups, chans, 2, pad, half), BF16),
+            pltpu.VMEM((groups, 2, chans, width, half), BF16),
             pltpu.VMEM((groups, train_dev, 2 * pad), BF16),
             pltpu.VMEM((rng_count, chans, train_dev, 2 * pad), BF16),
-            pltpu.VMEM((groups, beams, lanes), F32),
             *store,
             dma((groups,)),
             dma((groups,)),
@@ -406,13 +412,32 @@
             dma((rng_count, chans)),
             dma((rng_count, chans)),
             dma,
-            dma((groups,)),
+            dma((groups // chans, chans)),
             dma((groups,)),
         ],
         compiler_params=pltpu.CompilerParams(
             collective_id=0, has_side_effects=True, vmem_limit_bytes=56 * 1024 * 1024
         ),
     )(jnp.transpose(snapshots, (0, 1, 3, 2)), train_gates, guard_keep, beam_cells)
+    return pl.pallas_call(
+        write_out,
+        out_shape=tuple(jax.ShapeDtypeStruct(r.shape, r.dtype) for r in results),
+        in_specs=[pl.BlockSpec(memory_space=pltpu.VMEM)] * 2,
+        out_specs=(pl.BlockSpec(memory_space=pl.ANY), pl.BlockSpec(memory_space=pl.ANY)),
+        scratch_shapes=[dma((2,))],
+        compiler_params=pltpu.CompilerParams(vmem_limit_bytes=4 * 1024 * 1024),
+    )(*results)
+
+
+def write_out(beams_in, weights_in, beams_out, weights_out, sem):
+    copies = [
+        pltpu.make_async_copy(beams_in, beams_out, sem.at[0]),
+        pltpu.make_async_copy(weights_in, weights_out, sem.at[1]),
+    ]
+    for copy in copies:
+        copy.start()
+    for copy in copies:
+        copy.wait()
 
 
 def solution(mesh):

time: 25.1 us -> 21.6 us (0.86)
  local copies, waits for them, and re-layouts: 3.21 us -> 0 us
  Pallas kernels: 21.1 us -> 20.8 us
    unnamed x2 -> x0, local copies, waits for them, and re-layouts: 3.21 us -> none
    pallas_call x1, Pallas kernels: 21.1 us -> 20 us  [per_device(): pl.pallas_call(functools.partial(kernel, rng_count, chans, pad), out_shap...]
    pallas_call x0 -> x1, Pallas kernels: none -> 0.75 us  [per_device(): pl.pallas_call(write_out, out_shape=tuple((jax.ShapeDtypeStruct(r.shape,...]
where the time goes in v2:
time: 21.6 us; the launch traced here: 21.4 us
  Pallas kernels  20.8 us (96%)
  between operations  0.64 us (3%)
    pallas_call x1, Pallas kernels, per_device(): pl.pallas_call(functools.partial(kernel, rng_count, chans, pad), out_shap...  20 us
    pallas_call x1, Pallas kernels, per_device(): pl.pallas_call(write_out, out_shape=tuple((jax.ShapeDtypeStruct(r.shape,...  0.75 us

profile of v2, /device:TPU:0, one launch (start us, length us, event | category | flops | bytes accessed | tf_op | source)
XLA Modules:
  0.0 21.4 jit_solution(12092218122735863078)
XLA Ops:
  0.6 20.0 %shard_map.59 = (bf16[4,2,16,1024]{3,2,1,0:T(8,128)(2,1)S(1)}, f32[4,16,384]{2,1,0:T(8,128)S(1)}) custom-call(bf16[4,2,96,2048]{3,2,1,0:T(8,128)(2,1)} %bitcast.1, s32[4,16]{1,0:T(4,128)} %gates.1, s32[4,16]{1,0:T(4,128)} %guard.1, s32[4,16]{1,0:T(4,128)} %cells.1), custom_call_target="tpu_custom_call" | custom-call | tf_op jit(solution)/shard_map/pallas_call | solution.py:386
  20.7 0.7 %shard_map.60 = (bf16[4,2,16,1024]{3,2,1,0:T(8,128)(2,1)}, f32[4,16,384]{2,1,0:T(8,128)}) custom-call(bf16[4,2,16,1024]{3,2,1,0:T(8,128)(2,1)S(1)} %get-tuple-element.4.beams_in, f32[4,16,384]{2,1,0:T(8,128)S(1)} %get-tuple-element.5.weights_in), custom_call_target="tpu_custom_call" | custom-call | tf_op jit(solution)/shard_map/pallas_call | solution.py:422

commit v3 on v2

--- a/solution.py
+++ b/solution.py
@@ -188,15 +188,19 @@
     chans,
     pad,
     snap,
-    gates,
-    guard,
-    cells,
+    gates_in,
+    guard_in,
+    cells_in,
     out,
     weights_out,
     full,
     cube,
     piece,
     rows,
+    gates,
+    guard,
+    cells,
+    scalar_sem,
     *rest,
 ):
     store, sems = rest[:-9], rest[-9:]
@@ -212,12 +216,6 @@
     mine = spot * chans + chan
     cluster = place - spot
 
-    loads = []
-    for g in range(groups):
-        load = pltpu.make_async_copy(snap.at[g], full.at[g], full_sem.at[g])
-        load.start()
-        loads.append(load)
-
     barrier = pltpu.get_barrier_semaphore()
     for d in range(rng_count):
         for e in range(chans):
@@ -233,6 +231,20 @@
                 device_id_type=MESH,
             )
 
+    scalars = [
+        pltpu.make_async_copy(source, held, scalar_sem.at[n])
+        for n, (source, held) in enumerate(
+            ((gates_in, gates), (guard_in, guard), (cells_in, cells))
+        )
+    ]
+    for scalar in scalars:
+        scalar.start()
+    loads = []
+    for g in range(groups):
+        load = pltpu.make_async_copy(snap.at[g], full.at[g], full_sem.at[g])
+        load.start()
+        loads.append(load)
+
     own_start = pl.multiple_of(chan * half, LANES)
     owns = []
     for g in range(groups):
@@ -244,6 +256,8 @@
         own.start()
         owns.append(own)
     piece[...] = jnp.zeros_like(piece)
+    for scalar in scalars:
+        scalar.wait()
     steer = steer_rows(lambda k: cells[mine, k], beams, chans, width, pad)
 
     row = lax.broadcasted_iota(jnp.int32, (train_dev, LANES), 0)
@@ -391,9 +405,9 @@
         ),
         in_specs=[
             pl.BlockSpec(memory_space=pl.ANY),
-            pl.BlockSpec(memory_space=pltpu.SMEM),
-            pl.BlockSpec(memory_space=pltpu.SMEM),
-            pl.BlockSpec(memory_space=pltpu.SMEM),
+            pl.BlockSpec(memory_space=pl.ANY),
+            pl.BlockSpec(memory_space=pl.ANY),
+            pl.BlockSpec(memory_space=pl.ANY),
         ],
         out_specs=(
             pl.BlockSpec(memory_space=pltpu.VMEM),
@@ -404,6 +418,10 @@
             pltpu.VMEM((groups, 2, chans, width, half), BF16),
             pltpu.VMEM((groups, train_dev, 2 * pad), BF16),
             pltpu.VMEM((rng_count, chans, train_dev, 2 * pad), BF16),
+            pltpu.SMEM(train_gates.shape, jnp.int32),
+            pltpu.SMEM(guard_keep.shape, jnp.int32),
+            pltpu.SMEM(beam_cells.shape, jnp.int32),
+            dma((3,)),
             *store,
             dma((groups,)),
             dma((groups,)),

time: 21.6 us -> 21 us (0.972)
  Pallas kernels: 20.8 us -> 20.2 us
    pallas_call x1, Pallas kernels: 20 us -> 19.4 us  [per_device(): pl.pallas_call(functools.partial(kernel, rng_count, chans, pad), out_shap...]
where the time goes in v3:
time: 21 us; the launch traced here: 20.8 us
  Pallas kernels  20.2 us (96%)
  between operations  0.64 us (3%)
    pallas_call x1, Pallas kernels, per_device(): pl.pallas_call(functools.partial(kernel, rng_count, chans, pad), out_shap...  19.4 us
    pallas_call x1, Pallas kernels, per_device(): pl.pallas_call(write_out, out_shape=tuple((jax.ShapeDtypeStruct(r.shape,...  0.75 us

profile of v3, /device:TPU:0, one launch (start us, length us, event | category | flops | bytes accessed | tf_op | source)
XLA Modules:
  0.0 20.8 jit_solution(17093106202143379820)
XLA Ops:
  0.6 19.4 %shard_map.59 = (bf16[4,2,16,1024]{3,2,1,0:T(8,128)(2,1)S(1)}, f32[4,16,384]{2,1,0:T(8,128)S(1)}) custom-call(bf16[4,2,96,2048]{3,2,1,0:T(8,128)(2,1)} %bitcast.1, s32[4,16]{1,0:T(4,128)} %gates_in.1, s32[4,16]{1,0:T(4,128)} %guard_in.1, s32[4,16]{1,0:T(4,128)} %cells_in.1), custom_call_target="tpu_custom_call" | custom-call | tf_op jit(solution)/shard_map/pallas_call | solution.py:400
  20.1 0.7 %shard_map.60 = (bf16[4,2,16,1024]{3,2,1,0:T(8,128)(2,1)}, f32[4,16,384]{2,1,0:T(8,128)}) custom-call(bf16[4,2,16,1024]{3,2,1,0:T(8,128)(2,1)S(1)} %get-tuple-element.4.beams_in, f32[4,16,384]{2,1,0:T(8,128)S(1)} %get-tuple-element.5.weights_in), custom_call_target="tpu_custom_call" | custom-call | tf_op jit(solution)/shard_map/pallas_call | solution.py:440
